TPU v7x, 512 devices: a whole 4x8x8 slice. The times are simulated.
512 devices in a mesh: blk: 32 (over x_lo, y, core), col: 16 (over x_hi, z).
Axes of the slice: x: 4 (x_hi: 2, x_lo: 2; x = x_hi * 2 + x_lo), y: 8, z: 8, core: 2. Of those that a mesh axis runs over, the one named last changes fastest.
Arguments:
- documents: bfloat16 [24576, 768], P('blk'), may hold values from -6 to 6
- landmarks: bfloat16 [65536, 768], P(('blk', 'col')), may hold values from -6 to 6
- eigen_vectors: bfloat16 [65536, 256], P(('blk', 'col')), may hold values from -6 to 6
- land_degree: float32 [65536], P(('blk', 'col')), may hold values from 0.5 to 8
- eigen_values: float32 [256], replicated, may hold values from 0.005 to 0.05
- tile_mask: int32 [192, 512], P('blk'), may hold values from 0 to 1, as said below
- labels: int32 [24576], P(('blk', 'col')), may hold values from 0 to 999
Outputs:
- embedding: float32 [24576, 256], P(('blk', 'col'))
- centroids: float32 [1000, 256], replicated
Inputs may be any that keep to these rules, and one draw needn't show every extreme that they name: `tile_mask`: 1 marks a live tile of 128 documents by 128 landmarks; every document block has at least one live tile.
All inputs are finite; a program needn't handle non-finite values.
Results may differ from a plain program's by a relative error of at most 0.0041.
Values may be sent and summed in bfloat16 or wider, within the bound.
A program may use at most 64 MiB of HBM per device.

v0:
```python
import jax
import jax.numpy as jnp
from jax import lax
from jax.sharding import PartitionSpec as P

C = 1000
BLOCK = 128


def side_by_side(arrays, axis, dim, along):
    ends, at = ([], 0)
    for a in arrays[:-1]:
        at += a.shape[along]
        ends.append(at)
    both = jnp.concatenate(arrays, axis=along)
    return tuple(jnp.split(lax.all_gather(both, axis, axis=dim, tiled=True), ends, axis=along))


def split_up(value, dim, peers):
    shape = value.shape
    parts = value.reshape(*shape[:dim], peers, shape[dim] // peers, *shape[dim + 1 :])
    return jnp.moveaxis(parts, dim, 0)


def sent_and_summed(value, axis, dim):
    peers = lax.axis_size(axis)
    parts = lax.all_to_all(split_up(value, dim, peers), axis, 0, 0, tiled=True)
    return jnp.sum(parts, axis=0)


def in_one_piece(arrays, axis, dim, along):
    columns = [a.reshape(*a.shape[:along], -1) for a in arrays]
    both = jnp.concatenate(columns, axis=along)
    whole, at, outs = (sent_and_summed(both, axis, dim), 0, [])
    for a, column in zip(arrays, columns):
        share = whole[..., at : at + column.shape[along]]
        outs.append(share.reshape(*share.shape[:along], *a.shape[along:]))
        at += column.shape[along]
    return tuple(outs)


def body(documents, landmarks, eigen_vectors, land_degree, eigen_values, tile_mask, labels):
    inverse_width = 4.0 / documents.shape[1]
    land_rows = landmarks.shape[0]
    doc_rows = documents.shape[0]
    col_index = lax.axis_index("col")
    col_count = lax.axis_size("col")
    scaled = (
        eigen_vectors.astype(jnp.float32) * lax.rsqrt(land_degree)[:, None] / eigen_values[None, :]
    ).astype(jnp.bfloat16)
    doc_square = jnp.sum(jnp.square(documents.astype(jnp.float32)), 1)
    initial = (
        jnp.zeros((doc_rows, scaled.shape[1]), jnp.float32),
        jnp.zeros((doc_rows,), jnp.float32),
    )
    land_piece, vector_piece = side_by_side((landmarks, scaled), "blk", 0, 1)
    piece_rows = land_piece.shape[0]
    offsets = jnp.arange(piece_rows, dtype=jnp.int32)
    whole_rows = (
        offsets // land_rows * (land_rows * col_count) + col_index * land_rows + offsets % land_rows
    )
    live_cols = jnp.take(tile_mask, whole_rows // BLOCK, axis=1)

    def compute(state):
        land_square = jnp.sum(jnp.square(land_piece.astype(jnp.float32)), 1)
        products = jnp.einsum(
            "df,lf->dl", documents, land_piece, preferred_element_type=jnp.float32
        )
        keep = jnp.repeat(live_cols, BLOCK, axis=0).astype(jnp.float32)
        weights = (
            jnp.exp(inverse_width * (2.0 * products - doc_square[:, None] - land_square[None, :]))
            * keep
        )
        total = jnp.dot(
            weights.astype(jnp.bfloat16), vector_piece, preferred_element_type=jnp.float32
        )
        return (total, jnp.sum(weights, 1))

    projection, degree = lax.cond(jnp.any(live_cols > 0), compute, lambda state: state, initial)
    projection, degree = in_one_piece((projection, degree), "col", 0, 1)
    embedding = projection * lax.rsqrt(degree)[:, None]
    unit_rows = embedding * lax.rsqrt(jnp.sum(jnp.square(embedding), 1, keepdims=True) + 1e-06)
    one_hot = (jnp.arange(C, dtype=jnp.int32)[:, None] == labels[None, :]).astype(jnp.float32)
    partial_sums = jnp.dot(
        one_hot, unit_rows, precision=lax.Precision.HIGHEST, preferred_element_type=jnp.float32
    )
    centroids = lax.psum(partial_sums, ("blk", "col"))
    return (embedding, centroids)


def solution(mesh):
    placed = (
        P("blk", None),
        P(("blk", "col"), None),
        P(("blk", "col"), None),
        P(("blk", "col")),
        P(),
        P("blk", None),
        P(("blk", "col")),
    )
    return jax.shard_map(
        body, mesh=mesh, in_specs=placed, out_specs=(P(("blk", "col"), None), P()), check_vma=False
    )
```

profile of v0, /device:TPU:23, one launch (start us, length us, event | category | flops | bytes accessed | tf_op | source)
XLA Modules:
  0.0 429.9 jit_solution(15334240320638322248)
XLA Ops:
  7.2 0.0 copy-start.1
  7.2 0.0 all-gather.2.cloned.1.call-start
  7.2 0.7 rsqrt.15
  8.0 0.9 divide_convert_fusion
  8.9 1.7 pad_maximum_fusion.1
  10.6 0.0 all-gather.2.cloned.1.call-update
  10.6 0.0 all-reduce.2.cloned.1.call-start
  10.6 0.9 copy.11
  11.5 0.1 compare_select_fusion
  11.6 10.8 %gather_fusion = s32[4096,6]{1,0:T(8,128)S(1)} fusion(s32[6,512]{0,1:T(8,128)S(1)} %copy.11, s32[4096]{0:T(1024)S(1)} %broadcast_clamp_fusion), kind=kCustom, calls=%fused_computation | custom fusion | bytes 212992 | tf_op jit(solution)/shard_map/jit(_take)/gather | solution.py:62
  22.5 3.8 compare_reduce_fusion
  27.0 0.0 copy-done.1
  27.0 0.2 convert_element_type.29
  27.1 62.1 %all-gather.2.cloned.1.call-done = bf16[4096,1024]{1,0:T(8,128)(2,1)} async-done(((bf16[128,1024]{1,0:T(8,128)(2,1)}), bf16[4096,1024]{1,0:T(8,128)(2,1)}) %all-gather.2.cloned.1.call-update) | async-done | bytes 8388624 | tf_op jit(solution)/shard_map/all_gather | solution.py:16
  89.2 17.6 %conditional.1 = (f32[16,48,256]{2,1,0:T(8,128)S(1)}, f32[16,48,1]{2,1,0:T(8,128)S(1)}) conditional(s32[]{:T(128)} %convert_element_type.26, () %tuple.20, (bf16[4096,1024]{1,0:T(8,128)(2,1)}, bf16[768,768]{1,0:T(8,128)(2,1)S(1)}, f32[768,768]{1,0:T(8,128)S(1)}, s32[6,4096]{0,1:T(8,128)}) %tuple.37), branch_computations={%region_1.2_spmd, %region_2.6_spmd} | conditional | flops 6475106304 | bytes 65716268 | solution.py:79
  89.2 2.9 copy.12
  92.1 1.1 convert_element_type.19
  93.2 0.2 multiply_reduce_fusion.1
  93.4 4.4 %multiply_reduce_fusion = f32[4096]{0:T(1024)S(1)} fusion(bf16[4096,1024]{1,0:T(8,128)(2,1)} %get-tuple-element.17), kind=kLoop, calls=%fused_computation.2 | loop fusion | flops 9433088 | bytes 6307840 | tf_op jit(solution)/shard_map/cond/branch_1_fun/reduce_sum | solution.py:65
  97.8 6.9 %fusion = (f32[768]{0:T(1024)S(1)}, bf16[768,4096]{1,0:T(8,128)(2,1)S(1)}) fusion(f32[6,4096]{1,0:T(8,128)S(1)} %convert_element_type.19, f32[4096]{0:T(1024)S(1)} %multiply_reduce_fusion, f32[768]{0:T(1024)S(1)} %multiply_reduce_fusion.1, bf16[768,768]{1,0:T(8,128)(2,1)S(1)} %get-tuple-element.16, bf16[4096,1024]{1,0:T(8,128)(2,1)S(1)} %copy-done), kind=kOutput, calls=%fused_computation.3 | convolution fusion | flops 4853857280 | bytes 13917184 | tf_op jit(solution)/shard_map/cond/branch_1_fun/df,lf->dl/dot_general | solution.py:66
  104.7 1.8 fusion.4
  106.5 0.3 concatenate.17
  106.8 0.1 pad_maximum_fusion
  106.9 38.2 %all_to_all.5 = f32[16,48,257]{2,1,0:T(8,128)S(1)} all-to-all(f32[16,48,257]{2,1,0:T(8,128)S(1)} %pad_maximum_fusion), channel_id=1, replica_groups=mesh['blk'=32,'col'=16] {'col'}, dimensions={0} | all-to-all | bytes 1579008 | tf_op jit(solution)/shard_map/all_to_all | solution.py:27
  145.1 0.1 reduce_sum.46
  145.2 0.1 fusion.13
  145.3 0.2 multiply_reduce_fusion.2
  145.5 0.0 copy-start.2
  145.5 1.6 fusion.6
  147.1 0.0 all-reduce.2.cloned.1.call-update
  147.1 273.7 %all-reduce.2.cloned.1.call-done = f32[1000,256]{1,0:T(8,128)} async-done(((f32[1000,256]{1,0:T(8,128)}), f32[1000,256]{1,0:T(8,128)}) %all-reduce.2.cloned.1.call-update) | async-done | bytes 1024016 | tf_op jit(solution)/shard_map/psum | solution.py:87
  420.8 2.2 copy.21
  (8 shorter events, 0.0 us)
Async XLA Ops:
  7.2 19.8 %copy-start.1 = (bf16[768,768]{1,0:T(8,128)(2,1)S(1)}, bf16[768,768]{1,0:T(8,128)(2,1)}, u32[]{:S(2)}) copy-start(bf16[768,768]{1,0:T(8,128)(2,1)} %param.9) | copy-start | bytes 3538948
  7.2 82.0 %all-gather.2.cloned.1.call-start = ((), (), s32[]{:S(2)}) async-start(), calls=%async_computation.1 | async-start | bytes 8650752 | tf_op jit(solution)/shard_map/all_gather | solution.py:16
  10.6 410.2 %all-reduce.2.cloned.1.call-start = ((), (), s32[]{:S(2)}) async-start(), calls=%async_computation.2 | async-start | bytes 2048000 | tf_op jit(solution)/shard_map/psum | solution.py:87
  89.2 56.3 %copy-start.3 = (s32[48]{0:T(128)S(1)}, s32[48]{0:T(128)}, u32[]{:S(2)}) copy-start(s32[48]{0:T(128)} %param.15) | copy-start | bytes 580
  92.1 5.7 %copy-start = (bf16[4096,1024]{1,0:T(8,128)(2,1)S(1)}, bf16[4096,1024]{1,0:T(8,128)(2,1)}, u32[]{:S(2)}) copy-start(bf16[4096,1024]{1,0:T(8,128)(2,1)} %get-tuple-element.17) | copy-start | bytes 25165828 | tf_op jit(solution)/shard_map/cond
  145.5 277.5 %copy-start.2 = (f32[48,256]{1,0:T(8,128)}, f32[48,256]{1,0:T(8,128)S(1)}, u32[]{:S(2)}) copy-start(f32[48,256]{1,0:T(8,128)S(1)} %get-tuple-element.45) | copy-start | bytes 147460
Sparse Core Ops, SparseCore 0:
  10.7 78.4 all-gather.1
  147.2 273.4 all-reduce.1
where the time goes:
time: 430 us
  waiting for transfers between devices  336 us (78%)
  blocking collectives  38.2 us (9%)
  local copies, waits for them, and re-layouts  17.9 us (4%)
  between operations  14.8 us (3%)
  other arithmetic  12.7 us (3%)
  matrix products  10.3 us (2%)
    psum x1, waiting for transfers between devices, body(): centroids = lax.psum(partial_sums, ('blk', 'col'))  274 us
    all_gather x1, waiting for transfers between devices, side_by_side(): lax.all_gather(both, axis, axis=dim, tiled=True)  62.1 us
    all_to_all x1, blocking collectives, sent_and_summed(): parts = lax.all_to_all(split_up(value, dim, peers), axis, 0, 0, tiled=True)  38.2 us
    gather x1, local copies, waits for them, and re-layouts, body(): live_cols = jnp.take(tile_mask, whole_rows // BLOCK, axis=1)  10.8 us
  transfers between devices with their start and end apart: 2, of which 2 were waited for; matrix products, arithmetic and copies ran while one was open for 4% of the time, Pallas kernels for 0%

commit v1 on v0

--- a/solution.py
+++ b/solution.py
@@ -84,7 +84,9 @@
     partial_sums = jnp.dot(
         one_hot, unit_rows, precision=lax.Precision.HIGHEST, preferred_element_type=jnp.float32
     )
-    centroids = lax.psum(partial_sums, ("blk", "col"))
+    centroids = partial_sums
+    for mesh_axis in ("blk", "col"):
+        centroids = lax.psum(centroids, mesh_axis)
     return (embedding, centroids)
 
 

time: 430 us -> 552 us (1.28)
  the two profiles are of different devices: /device:TPU:23 before, /device:TPU:8 now
where the time goes in v1:
time: 552 us
  waiting for transfers between devices  454 us (82%)
  blocking collectives  42.5 us (8%)
  local copies, waits for them, and re-layouts  17.9 us (3%)
  between operations  14.5 us (3%)
  other arithmetic  12.7 us (2%)
  matrix products  10.3 us (2%)
    psum x2, waiting for transfers between devices, body(): centroids = lax.psum(centroids, mesh_axis)  392 us
    all_gather x1, waiting for transfers between devices, side_by_side(): lax.all_gather(both, axis, axis=dim, tiled=True)  61.7 us
    all_to_all x1, blocking collectives, sent_and_summed(): parts = lax.all_to_all(split_up(value, dim, peers), axis, 0, 0, tiled=True)  42.5 us
  transfers between devices with their start and end apart: 3, of which 3 were waited for; matrix products, arithmetic and copies ran while one was open for 3% of the time, Pallas kernels for 0%

profile of v1, /device:TPU:8, one launch (start us, length us, event | category | flops | bytes accessed | tf_op | source)
XLA Modules:
  0.0 551.9 jit_solution(13076691861495052865)
XLA Ops:
  7.2 0.0 all-gather.2.cloned.1.call-start
  7.2 0.7 rsqrt.15
  8.0 0.9 divide_convert_fusion
  8.9 1.7 pad_maximum_fusion.1
  10.6 0.0 all-gather.2.cloned.1.call-update
  10.6 0.0 all-reduce.3.cloned.1.call-start
  10.6 0.9 copy.11
  11.5 0.1 compare_select_fusion
  11.6 10.8 %gather_fusion = s32[4096,6]{1,0:T(8,128)S(1)} fusion(s32[6,512]{0,1:T(8,128)S(1)} %copy.11, s32[4096]{0:T(1024)S(1)} %broadcast_clamp_fusion), kind=kCustom, calls=%fused_computation | custom fusion | bytes 212992 | tf_op jit(solution)/shard_map/jit(_take)/gather | solution.py:62
  22.5 3.8 compare_reduce_fusion
  27.0 0.2 convert_element_type.29
  27.1 61.7 %all-gather.2.cloned.1.call-done = bf16[4096,1024]{1,0:T(8,128)(2,1)} async-done(((bf16[128,1024]{1,0:T(8,128)(2,1)}), bf16[4096,1024]{1,0:T(8,128)(2,1)}) %all-gather.2.cloned.1.call-update) | async-done | bytes 8388624 | tf_op jit(solution)/shard_map/all_gather | solution.py:16
  88.8 17.6 %conditional.1 = (f32[16,48,256]{2,1,0:T(8,128)S(1)}, f32[16,48,1]{2,1,0:T(8,128)S(1)}) conditional(s32[]{:T(128)} %convert_element_type.26, () %tuple.20, (bf16[4096,1024]{1,0:T(8,128)(2,1)}, bf16[768,768]{1,0:T(8,128)(2,1)S(1)}, f32[768,768]{1,0:T(8,128)S(1)}, s32[6,4096]{0,1:T(8,128)}) %tuple.39), branch_computations={%region_1.2_spmd, %region_2.6_spmd} | conditional | flops 6475106304 | bytes 65716268 | solution.py:79
  88.8 2.9 copy.12
  91.7 1.1 convert_element_type.19
  92.7 0.2 multiply_reduce_fusion.1
  93.0 4.4 multiply_reduce_fusion
  97.4 6.9 %fusion = (f32[768]{0:T(1024)S(1)}, bf16[768,4096]{1,0:T(8,128)(2,1)S(1)}) fusion(f32[6,4096]{1,0:T(8,128)S(1)} %convert_element_type.19, f32[4096]{0:T(1024)S(1)} %multiply_reduce_fusion, f32[768]{0:T(1024)S(1)} %multiply_reduce_fusion.1, bf16[768,768]{1,0:T(8,128)(2,1)S(1)} %get-tuple-element.16, bf16[4096,1024]{1,0:T(8,128)(2,1)S(1)} %copy-done), kind=kOutput, calls=%fused_computation.3 | convolution fusion | flops 4853857280 | bytes 13917184 | tf_op jit(solution)/shard_map/cond/branch_1_fun/df,lf->dl/dot_general | solution.py:66
  104.2 1.8 fusion.4
  106.1 0.3 concatenate.17
  106.4 0.1 pad_maximum_fusion
  106.5 42.5 %all_to_all.5 = f32[16,48,257]{2,1,0:T(8,128)S(1)} all-to-all(f32[16,48,257]{2,1,0:T(8,128)S(1)} %pad_maximum_fusion), channel_id=1, replica_groups=mesh['blk'=32,'col'=16] {'col'}, dimensions={0} | all-to-all | bytes 1579008 | tf_op jit(solution)/shard_map/all_to_all | solution.py:27
  149.0 0.1 reduce_sum.46
  149.1 0.1 fusion.13
  149.2 0.2 multiply_reduce_fusion.2
  149.4 1.6 fusion.6
  151.0 0.0 all-reduce.3.cloned.1.call-update
  151.0 0.0 all-reduce.5.cloned.1.call-start
  151.0 223.0 %all-reduce.3.cloned.1.call-done = f32[1000,256]{1,0:T(8,128)} async-done(((f32[1000,256]{1,0:T(8,128)}), f32[1000,256]{1,0:T(8,128)}) %all-reduce.3.cloned.1.call-update) | async-done | bytes 1024016 | tf_op jit(solution)/shard_map/psum | solution.py:89
  374.1 0.0 all-reduce.5.cloned.1.call-update
  374.1 169.1 %all-reduce.5.cloned.1.call-done = f32[1000,256]{1,0:T(8,128)} async-done(((f32[1000,256]{1,0:T(8,128)}), f32[1000,256]{1,0:T(8,128)}) %all-reduce.5.cloned.1.call-update) | async-done | bytes 1024016 | tf_op jit(solution)/shard_map/psum | solution.py:89
  543.2 2.2 copy.22
  (11 shorter events, 0.1 us)
Async XLA Ops:
  7.2 19.8 %copy-start.1 = (bf16[768,768]{1,0:T(8,128)(2,1)S(1)}, bf16[768,768]{1,0:T(8,128)(2,1)}, u32[]{:S(2)}) copy-start(bf16[768,768]{1,0:T(8,128)(2,1)} %param.9) | copy-start | bytes 3538948
  7.2 81.6 %all-gather.2.cloned.1.call-start = ((), (), s32[]{:S(2)}) async-start(), calls=%async_computation.1 | async-start | bytes 8650752 | tf_op jit(solution)/shard_map/all_gather | solution.py:16
  10.6 363.5 %all-reduce.3.cloned.1.call-start = ((), (), s32[]{:S(2)}) async-start(), calls=%async_computation.2 | async-start | bytes 2048000 | tf_op jit(solution)/shard_map/psum | solution.py:89
  88.8 60.6 %copy-start.3 = (s32[48]{0:T(128)S(1)}, s32[48]{0:T(128)}, u32[]{:S(2)}) copy-start(s32[48]{0:T(128)} %param.15) | copy-start | bytes 580
  91.7 5.7 %copy-start = (bf16[4096,1024]{1,0:T(8,128)(2,1)S(1)}, bf16[4096,1024]{1,0:T(8,128)(2,1)}, u32[]{:S(2)}) copy-start(bf16[4096,1024]{1,0:T(8,128)(2,1)} %get-tuple-element.17) | copy-start | bytes 25165828 | tf_op jit(solution)/shard_map/cond
  149.4 396.1 %copy-start.2 = (f32[48,256]{1,0:T(8,128)}, f32[48,256]{1,0:T(8,128)S(1)}, u32[]{:S(2)}) copy-start(f32[48,256]{1,0:T(8,128)S(1)} %get-tuple-element.45) | copy-start | bytes 147460
  151.0 392.2 %all-reduce.5.cloned.1.call-start = ((), (), s32[]{:S(2)}) async-start(), calls=%async_computation.3 | async-start | bytes 2048000 | tf_op jit(solution)/shard_map/psum | solution.py:89
Sparse Core Ops, SparseCore 0:
  10.7 78.0 all-gather.1
  151.1 222.9 all-reduce.2
  377.0 166.0 all-reduce.4
